TPU v7x, 32 devices: a 4x4x1 block of a 4x4x8 slice. The times are simulated.
32 devices in a mesh: dp: 2 (over z, core), tp: 16 (over x, y).
Axes of the slice: x: 4, y: 4, z: 1, core: 2. Of those that a mesh axis runs over, the one named last changes fastest.
The devices are a block of a 4x4x8 slice.
Arguments:
- x: bfloat16 [128, 2048], P('dp'), parts along dimension 0
- k_cache: bfloat16 [128, 4096, 16, 128], P('dp', None, 'tp'), parts along dimension 0
- v_cache: bfloat16 [128, 4096, 16, 128], P('dp', None, 'tp'), parts along dimension 0
- gain_a: bfloat16 [2048], replicated
- wq: bfloat16 [2048, 2048], P(None, 'tp')
- wo: bfloat16 [2048, 2048], P('tp')
- gain_m: bfloat16 [2048], replicated
- w_gate: bfloat16 [2048, 8192], P(None, 'tp')
- w_up: bfloat16 [2048, 8192], P(None, 'tp')
- w_down: bfloat16 [8192, 2048], P('tp')
Outputs:
- output: bfloat16 [128, 2048], P('dp'), parts along dimension 0
There are 2 independent parts. A program takes and returns all parts, laid end to end along the dimension named above; an argument that names none is the same for every part.
All inputs are finite; a program needn't handle non-finite values.
Results may differ from a plain program's by a relative error of at most 0.017.
Values are sent between devices in bfloat16 or wider.
A program may use at most 768 MiB of HBM per device.

v0:
```python
import jax
import jax.numpy as jnp
from jax import lax
from jax.sharding import PartitionSpec as P

HEAD = 128
THETA = 10000


def normed(x, gain):
    wide = x.astype(jnp.float32)
    scale = lax.rsqrt(jnp.mean(wide * wide, -1, keepdims=True) + 1e-6)
    return (wide * scale * gain.astype(jnp.float32)).astype(jnp.bfloat16)


def turned(t, place, theta):
    half = t.shape[-1] // 2
    angle = place.astype(jnp.float32)[:, None] * theta ** (-jnp.arange(half, dtype=jnp.float32) / half)
    cos, sin = jnp.cos(angle)[:, None], jnp.sin(angle)[:, None]
    a, b = t[..., :half].astype(jnp.float32), t[..., half:].astype(jnp.float32)
    return jnp.concatenate([a * cos - b * sin, b * cos + a * sin], -1).astype(jnp.bfloat16)


def matmul(a, w):
    return jnp.dot(a, w, preferred_element_type=jnp.float32).astype(jnp.bfloat16)


def einsum(form, a, b):
    return jnp.einsum(form, a.astype(jnp.float32), b.astype(jnp.float32))


def seen_by(a, wq, k_cache, v_cache, head, theta):
    batch, cache, kv_heads = k_cache.shape[:3]
    place = jnp.full((batch,), cache - 1)
    q = turned(matmul(a, wq).reshape(batch, -1, head), place, theta).reshape(batch, kv_heads, -1, head)
    scores = einsum("bgsd,bugd->bgsu", q, k_cache) * head**-0.5
    weights = jax.nn.softmax(scores, -1).astype(jnp.bfloat16)
    return einsum("bgsu,bugd->bgsd", weights, v_cache).astype(jnp.bfloat16).reshape(batch, -1)


def hidden_of(b, w_gate, w_up):
    gate = jnp.dot(b, w_gate, preferred_element_type=jnp.float32)
    up = jnp.dot(b, w_up, preferred_element_type=jnp.float32)
    return (jax.nn.silu(gate) * up).astype(jnp.bfloat16)


def solution(mesh):
    def added(t, term):
        return (t.astype(jnp.float32) + lax.psum(term.astype(jnp.bfloat16), "tp").astype(jnp.float32)).astype(jnp.bfloat16)

    def step(x, k_cache, v_cache, gain_a, wq, wo, gain_m, w_gate, w_up, w_down):
        seen = seen_by(normed(x, gain_a), wq, k_cache, v_cache, HEAD, THETA)
        h = added(x, jnp.dot(seen, wo, preferred_element_type=jnp.float32))
        return added(h, jnp.dot(hidden_of(normed(h, gain_m), w_gate, w_up), w_down, preferred_element_type=jnp.float32))

    states, cache, columns, rows_of = P("dp", None), P("dp", None, "tp", None), P(None, "tp"), P("tp", None)
    return jax.shard_map(
        step,
        mesh=mesh,
        in_specs=(states, cache, cache, P(None), columns, rows_of, P(None), columns, columns, rows_of),
        out_specs=states,
        check_vma=False,
    )
```

profile of v0, /device:TPU:96, one launch (start us, length us, event | category | flops | bytes accessed | tf_op | source)
XLA Modules:
  0.0 227.8 jit_solution(5136649129156587849)
XLA Ops:
  6.5 0.0 copy-start
  6.6 0.0 all-reduce.3.cloned.1.call-start
  6.6 0.8 convert_element_type.68
  7.4 1.1 fusion.9
  8.6 1.4 fusion.5
  10.0 0.1 fusion.37
  10.1 0.1 maximum_bitcast_fusion
  10.1 25.3 %fusion.2 = f32[64,1,4096]{2,1,0:T(1,128)S(1)} fusion(bf16[64,4096,1,128]{3,1,2,0:T(8,128)(2,1)} %param.11, bf16[64,128,1]{1,0,2:T(8,128)(2,1)S(1)} %maximum_bitcast_fusion), kind=kOutput, calls=%fused_computation.2 | convolution fusion | flops 67108864 | bytes 68173824 | tf_op jit(solution)/shard_map/bgsd,bugd->bgsu/dot_general | solution.py:29
  35.5 0.8 fusion.8
  36.3 0.8 fusion.7
  37.0 0.8 fusion.17
  37.9 0.0 copy-start.2
  37.9 0.0 copy-start.3
  37.9 0.0 copy-start.1
  37.9 22.7 %fusion = f32[64,1,128]{2,1,0:T(1,128)S(1)} fusion(bf16[64,4096,1,128]{3,1,2,0:T(8,128)(2,1)} %param.12, bf16[64,4096,1]{1,0,2:T(8,128)(2,1)S(1)} %fusion.17), kind=kOutput, calls=%fused_computation | convolution fusion | flops 67108864 | bytes 67665920 | tf_op jit(solution)/shard_map/bgsu,bugd->bgsd/dot_general | solution.py:29
  60.7 0.0 copy-done.2
  60.7 0.9 convolution_convert_fusion.1
  61.6 0.1 all-reduce.3.cloned.1.call-update
  61.6 0.1 all-reduce.5.cloned.1.call-start
  61.7 0.0 copy-done.3
  61.7 77.0 %all-reduce.3.cloned.1.call-done = bf16[64,2048]{1,0:T(8,128)(2,1)} async-done(((bf16[64,2048]{1,0:T(8,128)(2,1)}), bf16[64,2048]{1,0:T(8,128)(2,1)}) %all-reduce.3.cloned.1.call-update) | async-done | bytes 262160 | tf_op jit(solution)/shard_map/psum | solution.py:49
  138.7 0.0 copy-done.1
  138.7 1.1 fusion.13
  139.9 2.1 fusion.28
  142.0 0.0 copy-done
  142.0 3.3 %convolution_convert_fusion = bf16[64,2048]{1,0:T(8,128)(2,1)} fusion(bf16[512,2048]{1,0:T(8,128)(2,1)S(1)} %copy-done, bf16[2048,512]{1,0:T(8,128)(2,1)} %param.18, f32[64,512]{1,0:T(8,128)S(1)} %fusion.28, bf16[64,2048]{1,0:T(8,128)(2,1)S(1)} %get-tuple-element.6, f32[2048]{0:T(1024)S(1)} %convert_element_type.79, f32[64]{0:T(128)S(1)} %add_rsqrt_fusion), kind=kOutput, calls=%fused_computation.4 | convolution fusion | flops 269287424 | bytes 4858112 | tf_op jit(solution)/shard_map/dot_general | solution.py:54
  145.3 0.1 all-reduce.5.cloned.1.call-update
  145.3 73.9 %all-reduce.5.cloned.1.call-done = bf16[64,2048]{1,0:T(8,128)(2,1)} async-done(((bf16[64,2048]{1,0:T(8,128)(2,1)}), bf16[64,2048]{1,0:T(8,128)(2,1)}) %all-reduce.5.cloned.1.call-update) | async-done | bytes 262160 | tf_op jit(solution)/shard_map/psum | solution.py:49
  219.2 1.7 fusion.16
  (4 shorter events, 0.1 us)
Async XLA Ops:
  6.5 135.4 %copy-start = (bf16[512,2048]{1,0:T(8,128)(2,1)S(1)}, bf16[512,2048]{1,0:T(8,128)(2,1)}, u32[]{:S(2)}) copy-start(bf16[512,2048]{1,0:T(8,128)(2,1)} %param.19) | copy-start | bytes 6291460
  6.6 132.2 %all-reduce.3.cloned.1.call-start = ((), (), s32[]{:S(2)}) async-start(), calls=%async_computation | async-start | bytes 524288 | tf_op jit(solution)/shard_map/psum | solution.py:49
  37.9 22.8 %copy-start.2 = (bf16[128,2048]{1,0:T(8,128)(2,1)S(1)}, bf16[128,2048]{1,0:T(8,128)(2,1)}, u32[]{:S(2)}) copy-start(bf16[128,2048]{1,0:T(8,128)(2,1)} %param.15) | copy-start | bytes 1572868
  37.9 23.8 %copy-start.3 = (bf16[2048]{0:T(1024)(128)(2,1)S(1)}, bf16[2048]{0:T(1024)(128)(2,1)}, u32[]{:S(2)}) copy-start(bf16[2048]{0:T(1024)(128)(2,1)} %param.16) | copy-start | bytes 12292
  37.9 100.8 %copy-start.1 = (bf16[64,2048]{1,0:T(8,128)(2,1)S(1)}, bf16[64,2048]{1,0:T(8,128)(2,1)}, u32[]{:S(2)}) copy-start(bf16[64,2048]{1,0:T(8,128)(2,1)} %param.10) | copy-start | bytes 786436
  61.6 157.5 %all-reduce.5.cloned.1.call-start = ((), (), s32[]{:S(2)}) async-start(), calls=%async_computation.1 | async-start | bytes 524288 | tf_op jit(solution)/shard_map/psum | solution.py:49
Sparse Core Ops, SparseCore 0:
  61.8 76.8 all-reduce.2
  145.4 73.7 all-reduce.4
where the time goes:
time: 228 us
  waiting for transfers between devices  151 us (66%)
  matrix products  55.8 us (24%)
  between operations  13.5 us (6%)
  other arithmetic  7.41 us (3%)
    psum x2, waiting for transfers between devices, added(): lax.psum(term.astype(jnp.bfloat16), 'tp').astype(jnp.float32)  151 us
    dot_general x2, matrix products, einsum(): return jnp.einsum(form, a.astype(jnp.float32), b.astype(jnp.float32))  48.1 us
  transfers between devices with their start and end apart: 2, of which 2 were waited for; matrix products, arithmetic and copies ran while one was open for 0% of the time, Pallas kernels for 0%

commit v1 on v0

v1 whole, which is shorter than its diff:
```python
import functools

import jax
import jax.numpy as jnp
import numpy as np
from jax import lax
from jax.experimental import pallas as pl
from jax.experimental.pallas import tpu as pltpu
from jax.sharding import PartitionSpec as P

HEAD = 128
THETA = 10000
GROUP = 16
PART = 4
SLOTS = 6
BLOCK = 256
UNIT = 8


F32, BF16 = jnp.float32, jnp.bfloat16


def scaled(wide, gain):
    scale = lax.rsqrt(jnp.mean(wide * wide, -1, keepdims=True) + 1e-6)
    return (wide * scale * gain.astype(F32)).astype(BF16)


def dot(a, b):
    return jnp.dot(a, b, preferred_element_type=F32)


def layer(
    side, cache,
    x_hbm, gain_a_hbm, gain_m_hbm, turn_hbm, wq_hbm, wo_hbm, wg_hbm, wu_hbm, wd_hbm, k_hbm, v_hbm,
    y_hbm,
    x_ref, gain_a_ref, gain_m_ref, turn_ref, wq_ref, wo_ref, wg_ref, wu_ref, wd_ref,
    ring, qd, s_ref, p_ref, part_o, h_ref, b_ref, y_ref, first, second,
    in_sem, ring_sem, out_sem, send_sem, recv_sem,
):
    units, _, d = x_ref.shape
    batch = units * UNIT
    half = d // 2
    rows = PART * cache
    per = GROUP // PART
    groups = batch // GROUP
    steps = groups * 2 * per
    me = lax.axis_index("tp")
    mx, my = me // side, me % side
    peers_x = [lax.rem(mx + i, side) * side + my for i in range(1, side)]
    peers_y = [mx * side + lax.rem(my + i, side) for i in range(1, side)]

    barrier = pltpu.get_barrier_semaphore()
    for peer in peers_x + peers_y:
        pl.semaphore_signal(barrier, inc=1, device_id={"tp": peer}, device_id_type=pl.DeviceIdType.MESH)

    def chunk(t, issue):
        g, c = t // (2 * per), t % (2 * per)
        slot = t % SLOTS

        @pl.when(c < per)
        def _():
            copy = pltpu.make_async_copy(k_hbm.at[pl.ds((g * per + c) * rows, rows)], ring.at[slot], ring_sem.at[slot])
            copy.start() if issue else copy.wait()

        @pl.when(c >= per)
        def _():
            copy = pltpu.make_async_copy(v_hbm.at[pl.ds((g * per + c - per) * rows, rows)], ring.at[slot], ring_sem.at[slot])
            copy.start() if issue else copy.wait()

    early = [(x_hbm, x_ref), (gain_a_hbm, gain_a_ref), (gain_m_hbm, gain_m_ref), (turn_hbm, turn_ref), (wq_hbm, wq_ref)]
    late = [(wo_hbm, wo_ref), (wg_hbm, wg_ref), (wu_hbm, wu_ref), (wd_hbm, wd_ref)]
    copies = [pltpu.make_async_copy(a, b, in_sem.at[i]) for i, (a, b) in enumerate(early + late)]
    for copy in copies[:len(early)]:
        copy.start()
    for t in range(SLOTS):
        chunk(t, True)
    for copy in copies[len(early):]:
        copy.start()
    for copy in copies[:len(early)]:
        copy.wait()

    a = scaled(x_ref[...].astype(F32).reshape(batch, d), gain_a_ref[...])
    q = dot(a, wq_ref[...]).astype(BF16).astype(F32)
    q = q * turn_ref[0:1, :] + pltpu.roll(q, HEAD // 2, 1) * turn_ref[1:2, :]
    row = lax.broadcasted_iota(jnp.int32, (GROUP, HEAD), 0)
    for g in range(groups):
        for s in range(GROUP):
            mine = jnp.where(row == s, q[g * GROUP:(g + 1) * GROUP], 0.0).astype(BF16)
            qd[g * per + s // PART, :, (s % PART) * HEAD:(s % PART + 1) * HEAD] = mine
    s_ref[...] = jnp.zeros_like(s_ref)
    pl.semaphore_wait(barrier, 2 * (side - 1))

    def side_by_side(buf, at):
        return jnp.concatenate([buf[pl.ds(i * cache + at, BLOCK), :] for i in range(PART)], axis=1)

    def spread(buf, n, u, hop, along_x, along_y, term):
        for slot, value, peers in ((along_x, term[0], peers_x), (along_y, term[1], peers_y)):
            buf[n, u, slot] = value.astype(BF16)
        for slot, peers in ((along_x, peers_x), (along_y, peers_y)):
            for peer in peers:
                pltpu.make_async_remote_copy(
                    src_ref=buf.at[n, u, slot], dst_ref=buf.at[n, u, slot],
                    send_sem=send_sem.at[n, u, hop], recv_sem=recv_sem.at[n, u, hop],
                    device_id={"tp": peer}, device_id_type=pl.DeviceIdType.MESH,
                ).start()

    def landed(buf, n, u, hop, sem):
        all_of_it = buf.at[n, u, pl.ds(0, 2 * (side - 1))]
        pltpu.make_async_copy(all_of_it, all_of_it, sem.at[n, u, hop]).wait()

    def total(buf, n, u, start):
        t = buf[n, u, start].astype(F32)
        for i in range(1, side):
            t = t + buf[n, u, start + i].astype(F32)
        return t

    def send_terms(n, u, term):
        spread(first, n, u, 0, mx, side + my, (term[:, :half], term[:, half:]))

    def send_sums(n, u):
        landed(first, n, u, 0, recv_sem)
        spread(second, n, u, 1, side + mx, my, (total(first, n, u, side), total(first, n, u, 0)))

    def summed(n, u):
        landed(second, n, u, 1, recv_sem)
        return jnp.concatenate([total(second, n, u, 0), total(second, n, u, side)], axis=1)

    def project(u):
        send_terms(0, u, dot((part_o[0] + part_o[1]).astype(BF16), wo_ref[...]))

    def middle(u):
        h = (x_ref[u].astype(F32) + summed(0, u)).astype(BF16)
        h_ref[u] = h
        b_ref[u] = scaled(h.astype(F32), gain_m_ref[...])

    def mlp(b):
        gate, up = dot(b, wg_ref[...]), dot(b, wu_ref[...])
        return dot((jax.nn.silu(gate) * up).astype(BF16), wd_ref[...])

    def written(u):
        return pltpu.make_async_copy(y_ref.at[u], y_hbm.at[u], out_sem.at[u])

    def finish(u):
        y_ref[u] = (h_ref[u].astype(F32) + summed(1, u)).astype(BF16)
        written(u).start()

    def step(t, carry):
        g, c = t // (2 * per), t % (2 * per)
        slot = t % SLOTS
        chunk(t, False)
        buf = ring.at[slot]

        @pl.when(c < per)
        def _():
            lhs = qd[g * per + c]
            for at in range(0, cache, BLOCK):
                s_ref[:, at:at + BLOCK] += lax.dot_general(
                    lhs, side_by_side(buf, at), (((1,), (1,)), ((), ())), preferred_element_type=F32)

        @pl.when(c >= per)
        def _():
            j = c - per
            acc = jnp.zeros((GROUP, PART * HEAD), F32)
            for at in range(0, cache, BLOCK):
                acc += dot(p_ref[:, at:at + BLOCK], side_by_side(buf, at))
            o = jnp.zeros((GROUP, HEAD), F32)
            for i in range(PART):
                o = jnp.where(row == j * PART + i, acc[:, i * HEAD:(i + 1) * HEAD], o)
            part_o[j % 2] = o[:UNIT] + o[UNIT:]

        @pl.when(t + SLOTS < steps)
        def _():
            chunk(t + SLOTS, True)

        @pl.when(c == per - 1)
        def _():
            scores = s_ref[...] * HEAD**-0.5
            e = jnp.exp(scores - jnp.max(scores, -1, keepdims=True))
            p_ref[...] = (e * (1 / jnp.sum(e, -1, keepdims=True))).astype(BF16)
            s_ref[...] = jnp.zeros_like(s_ref)

        @pl.when(t == per)
        def _():
            for copy in copies[len(early):]:
                copy.wait()

        @pl.when((c == per + 1) | (c == per + 3))
        def _():
            project(2 * g + (c - per) // 2)

        @pl.when((c == 1) & (g > 0))
        def _():
            for i in range(2):
                send_sums(0, 2 * g - 2 + i)

        @pl.when((c == 3) & (g > 0))
        def _():
            for i in range(2):
                middle(2 * g - 2 + i)

        @pl.when((c == 4) & (g > 0))
        def _():
            term = mlp(b_ref[pl.ds(2 * g - 2, 2)].astype(F32).reshape(GROUP, d).astype(BF16))
            for i in range(2):
                send_terms(1, 2 * g - 2 + i, term[i * UNIT:(i + 1) * UNIT])

        @pl.when((c == 7) & (g > 0) & (g < groups - 1))
        def _():
            for i in range(2):
                send_sums(1, 2 * g - 2 + i)

        @pl.when((c == 2) & (g > 1))
        def _():
            for i in range(2):
                finish(2 * g - 4 + i)

        return carry

    lax.fori_loop(0, steps, step, 0)

    e, f = units - 2, units - 1
    send_sums(0, e)
    send_sums(1, e - 2)
    send_sums(1, e - 1)
    send_sums(0, f)
    middle(e)
    send_terms(1, e, mlp(b_ref[e]))
    finish(e - 2)
    finish(e - 1)
    middle(f)
    send_terms(1, f, mlp(b_ref[f]))
    send_sums(1, e)
    send_sums(1, f)
    finish(e)
    finish(f)

    def drain(u, carry):
        written(u).wait()
        for n in range(2):
            landed(first, n, u, 0, send_sem)
            landed(second, n, u, 1, send_sem)
        return carry

    lax.fori_loop(0, units, drain, 0)


def turn_table(cache):
    half = HEAD // 2
    angle = (cache - 1) * float(THETA) ** (-np.arange(half) / half)
    cos, sin = np.cos(angle), np.sin(angle)
    table = np.zeros((8, HEAD), np.float32)
    table[0] = np.concatenate([cos, cos])
    table[1] = np.concatenate([-sin, sin])
    return table


def solution(mesh):
    devices = mesh.shape["tp"]
    side = int(devices**0.5)

    def step(x, k_cache, v_cache, gain_a, wq, wo, gain_m, w_gate, w_up, w_down):
        batch, cache = k_cache.shape[:2]
        d = x.shape[1]
        units = batch // UNIT
        hbm = pl.BlockSpec(memory_space=pltpu.HBM)
        operands = (
            x.reshape(units, UNIT, d), gain_a.reshape(1, d), gain_m.reshape(1, d), turn_table(cache),
            wq, wo, w_gate, w_up, w_down, k_cache.reshape(batch * cache, HEAD), v_cache.reshape(batch * cache, HEAD),
        )
        buffers = pltpu.VMEM((2, units, 2 * side, UNIT, d // 2), BF16)
        y = pl.pallas_call(
            functools.partial(layer, side, cache),
            name="layer",
            out_shape=jax.ShapeDtypeStruct((units, UNIT, d), BF16),
            in_specs=[hbm] * len(operands),
            out_specs=hbm,
            scratch_shapes=[pltpu.VMEM(t.shape, t.dtype) for t in operands[:-2]] + [
                pltpu.VMEM((SLOTS, PART * cache, HEAD), BF16),
                pltpu.VMEM((batch // PART, GROUP, PART * HEAD), BF16),
                pltpu.VMEM((GROUP, cache), F32),
                pltpu.VMEM((GROUP, cache), BF16),
                pltpu.VMEM((2, UNIT, HEAD), F32),
                pltpu.VMEM((units, UNIT, d), BF16),
                pltpu.VMEM((units, UNIT, d), BF16),
                pltpu.VMEM((units, UNIT, d), BF16),
                buffers,
                buffers,
                pltpu.SemaphoreType.DMA((len(operands) - 2,)),
                pltpu.SemaphoreType.DMA((SLOTS,)),
                pltpu.SemaphoreType.DMA((units,)),
                pltpu.SemaphoreType.DMA((2, units, 2)),
                pltpu.SemaphoreType.DMA((2, units, 2)),
            ],
            compiler_params=pltpu.CompilerParams(collective_id=0, has_side_effects=True, vmem_limit_bytes=58 * 2**20),
        )(*operands)
        return y.reshape(batch, d)

    states, cache, columns, rows_of = P("dp", None), P("dp", None, "tp", None), P(None, "tp"), P("tp", None)
    return jax.shard_map(
        step,
        mesh=mesh,
        in_specs=(states, cache, cache, P(None), columns, rows_of, P(None), columns, columns, rows_of),
        out_specs=states,
        check_vma=False,
    )
```

time: 228 us -> 77.2 us (0.34)
  waiting for transfers between devices: 151 us -> 0 us
  Pallas kernels: 0 us -> 72.8 us
  matrix products: 55.8 us -> 0 us
  between operations: 13.5 us -> 0.01 us
  other arithmetic: 7.41 us -> 0 us
  local copies, waits for them, and re-layouts: 0.02 us -> 4.24 us
    psum x2 -> x0, waiting for transfers between devices: 151 us -> none  [added(): lax.psum(term.astype(jnp.bfloat16), 'tp').astype(jnp.float32)]
    pallas_call x0 -> x1, Pallas kernels: none -> 72.8 us  [step(): pl.pallas_call(functools.partial(layer, side, cache), name='layer', out_s...]
    dot_general x6 -> x0, matrix products: 55.8 us -> none  [the longest x2 48.1 us: einsum(): return jnp.einsum(form, a.astype(jnp.float32), b.astype(jnp.float32))]
    convert_element_type x4 -> x0, other arithmetic: 3.38 us -> none  [the longest x1 1.71 us: added(): (t.astype(jnp.float32) + lax.psum(term.astype(jnp.bfloat16), 'tp').astype...]
    reduce_sum x3 -> x0, other arithmetic: 3.03 us -> none  [the longest x2 2.24 us: normed(): scale = lax.rsqrt(jnp.mean(wide * wide, -1, keepdims=True) + 1e-06)]
    reshape x0 -> x2, local copies, waits for them, and re-layouts: none -> 2.57 us  [the longest x1 1.29 us: step(): gain_a.reshape(1, d)]
  transfers between devices with their start and end apart: 2 -> 0, of which waited for: 2 -> 0; matrix products, arithmetic and copies ran while one was open for 0% -> 0% of each run, Pallas kernels for 0% -> 0%
where the time goes in v1:
time: 77.2 us; the launch traced here: 77 us
  Pallas kernels  72.8 us (94%)
  local copies, waits for them, and re-layouts  4.24 us (5%)
    pallas_call x1, Pallas kernels, step(): pl.pallas_call(functools.partial(layer, side, cache), name='layer', out_s...  72.8 us
    unnamed x1, local copies, waits for them, and re-layouts  1.67 us

profile of v1, /device:TPU:96, one launch (start us, length us, event | category | flops | bytes accessed | tf_op | source)
XLA Modules:
  0.0 77.0 jit_solution(3432428328001632436)
XLA Ops:
  0.0 1.3 %reshape.19.gain_a_hbm = bf16[1,2048]{1,0:T(2,128)(2,1)} reshape(bf16[2048]{0:T(1024)(128)(2,1)} %param.14) | data formatting | bytes 8192 | tf_op jit(solution)/shard_map/reshape | solution.py:267
  1.3 1.3 %reshape.20.gain_m_hbm = bf16[1,2048]{1,0:T(2,128)(2,1)} reshape(bf16[2048]{0:T(1024)(128)(2,1)} %param.17) | data formatting | bytes 8192 | tf_op jit(solution)/shard_map/reshape | solution.py:267
  2.6 72.8 %layer.1 = bf16[8,8,2048]{2,1,0:T(8,128)(2,1)} custom-call(bf16[8,8,2048]{2,1,0:T(8,128)(2,1)} %bitcast.5, bf16[1,2048]{1,0:T(2,128)(2,1)} %reshape.19.gain_a_hbm, bf16[1,2048]{1,0:T(2,128)(2,1)} %reshape.20.gain_m_hbm, f32[8,128]{1,0:T(8,128)} %constant.2.clone.turn_hbm, bf16[2048,128]{1,0:T(8,128)(2,1)} %wq_hbm.1, bf16[128,2048]{1,0:T(8,128)(2,1)} %wo_hbm.1, ...), custom_call_target="tpu_custom_call" | custom-call | tf_op jit(solution)/shard_map/layer/pallas_call | solution.py:271
  75.4 1.7 %copy.13 = bf16[64,2048]{1,0:T(8,128)(2,1)} copy(bf16[64,2048]{1,0:T(8,128)(2,1)} %bitcast.4) | data formatting | bytes 524288

commit v2 on v1

v2 whole, which is shorter than its diff:
```python
import functools

import jax
import jax.numpy as jnp
import numpy as np
from jax import lax
from jax.experimental import pallas as pl
from jax.experimental.pallas import tpu as pltpu
from jax.sharding import PartitionSpec as P

HEAD = 128
THETA = 10000
PART = 4
CHUNKS = 4
AHEAD = 2
BLOCK = 256
UNIT = 8


F32, BF16 = jnp.float32, jnp.bfloat16


def scaled(wide, gain):
    scale = lax.rsqrt(jnp.mean(wide * wide, -1, keepdims=True) + 1e-6)
    return (wide * scale * gain.astype(F32).reshape(1, -1)).astype(BF16)


def dot(a, b):
    return jnp.dot(a, b, preferred_element_type=F32)


def layer(
    side, cache,
    x_hbm, gain_a_hbm, gain_m_hbm, turn_hbm, wq_hbm, wo_hbm, wg_hbm, wu_hbm, wd_hbm, k_hbm, v_hbm,
    y_ref,
    x_ref, gain_a_ref, gain_m_ref, turn_ref, wq_ref, wo_ref, wg_ref, wu_ref, wd_ref,
    ring, qd, s_ref, p_ref, part_o, h_ref, b_ref, first, second,
    in_sem, ring_sem, send_sem, recv_sem,
):
    units, _, d = x_ref.shape
    batch = units * UNIT
    half = d // 2
    rows = PART * cache
    me = lax.axis_index("tp")
    mx, my = me // side, me % side
    hops = sorted(range(1, side), key=lambda i: -min(i, side - i))
    peers_x = [lax.rem(mx + i, side) * side + my for i in hops]
    peers_y = [mx * side + lax.rem(my + i, side) for i in hops]

    barrier = pltpu.get_barrier_semaphore()
    for peer in peers_x + peers_y:
        pl.semaphore_signal(barrier, inc=1, device_id={"tp": peer}, device_id_type=pl.DeviceIdType.MESH)

    def chunk(u, c):
        slot = lax.rem(u, AHEAD) * CHUNKS + c
        return pltpu.make_async_copy((k_hbm, v_hbm)[c // 2].at[pl.ds((2 * u + c % 2) * rows, rows)], ring.at[slot], ring_sem.at[slot])

    def refill(u, c):
        @pl.when(u + AHEAD < units)
        def _():
            chunk(u + AHEAD, c).start()

    early = [(x_hbm, x_ref), (gain_a_hbm, gain_a_ref), (gain_m_hbm, gain_m_ref), (turn_hbm, turn_ref), (wq_hbm, wq_ref), (wo_hbm, wo_ref)]
    late = [(wg_hbm, wg_ref), (wu_hbm, wu_ref), (wd_hbm, wd_ref)]
    copies = [pltpu.make_async_copy(a, b, in_sem.at[i]) for i, (a, b) in enumerate(early + late)]
    for copy in copies[:len(early) - 1]:
        copy.start()
    for c in range(2):
        chunk(0, c).start()
    for copy in copies[:len(early) - 1]:
        copy.wait()
    copies[len(early) - 1].start()
    for t in range(2, AHEAD * CHUNKS):
        chunk(t // CHUNKS, t % CHUNKS).start()
    for copy in copies[len(early):]:
        copy.start()

    a = scaled(x_ref[...].astype(F32).reshape(batch, d), gain_a_ref[...])
    q = dot(a, wq_ref[...]).astype(BF16).astype(F32)
    q = q * turn_ref[0:1, :] + pltpu.roll(q, HEAD // 2, 1) * turn_ref[1:2, :]
    row = lax.broadcasted_iota(jnp.int32, (UNIT, HEAD), 0)
    for u in range(units):
        for i in range(UNIT):
            qd[u, :, i * HEAD:(i + 1) * HEAD] = jnp.where(row == i, q[u * UNIT:(u + 1) * UNIT], 0.0).astype(BF16)
    pl.semaphore_wait(barrier, 2 * (side - 1))

    def side_by_side(u, chunks, at):
        bufs = [ring.at[lax.rem(u, AHEAD) * CHUNKS + c] for c in chunks]
        return jnp.concatenate([buf[pl.ds(i * cache + at, BLOCK), :] for buf in bufs for i in range(PART)], axis=1)

    def score(u, chunks):
        c = chunks[0] % 2 * PART * HEAD
        lhs = qd[u, :, c:c + len(chunks) * PART * HEAD]
        return [
            lax.dot_general(lhs, side_by_side(u, chunks, at), (((1,), (1,)), ((), ())), preferred_element_type=F32)
            for at in range(0, cache, BLOCK)
        ]

    def weigh():
        scores = s_ref[...] * HEAD**-0.5
        e = jnp.exp(scores - jnp.max(scores, -1, keepdims=True))
        p_ref[...] = (e * (1 / jnp.sum(e, -1, keepdims=True))).astype(BF16)

    def mixed(u, chunks):
        acc = jnp.zeros((UNIT, len(chunks) * PART * HEAD), F32)
        for at in range(0, cache, BLOCK):
            acc += dot(p_ref[:, at:at + BLOCK], side_by_side(u, chunks, at))
        o = jnp.zeros((UNIT, HEAD), F32)
        for i in range(len(chunks) * PART):
            o = jnp.where(row == chunks[0] % 2 * PART + i, acc[:, i * HEAD:(i + 1) * HEAD], o)
        return o

    def spread(buf, n, u, hop, along_x, along_y, term):
        for slot, value, peers in ((along_x, term[0], peers_x), (along_y, term[1], peers_y)):
            buf[n, u, slot] = value.astype(BF16)
        for slot, peers in ((along_x, peers_x), (along_y, peers_y)):
            for peer in peers:
                pltpu.make_async_remote_copy(
                    src_ref=buf.at[n, u, slot], dst_ref=buf.at[n, u, slot],
                    send_sem=send_sem.at[n, u, hop], recv_sem=recv_sem.at[n, u, hop],
                    device_id={"tp": peer}, device_id_type=pl.DeviceIdType.MESH,
                ).start()

    def landed(buf, n, u, hop, sem):
        all_of_it = buf.at[n, u, pl.ds(0, 2 * (side - 1))]
        pltpu.make_async_copy(all_of_it, all_of_it, sem.at[n, u, hop]).wait()

    def total(buf, n, u, start):
        t = buf[n, u, start].astype(F32)
        for i in range(1, side):
            t = t + buf[n, u, start + i].astype(F32)
        return t

    def send_terms(n, u, term):
        spread(first, n, u, 0, mx, side + my, (term[:, :half], term[:, half:]))

    def send_sums(n, u):
        landed(first, n, u, 0, recv_sem)
        spread(second, n, u, 1, side + mx, my, (total(first, n, u, side), total(first, n, u, 0)))

    def summed(n, u):
        landed(second, n, u, 1, recv_sem)
        return jnp.concatenate([total(second, n, u, 0), total(second, n, u, side)], axis=1)

    def project(u, o):
        send_terms(0, u, dot(o.astype(BF16), wo_ref[...]))

    def middle(u):
        h = (x_ref[u].astype(F32) + summed(0, u)).astype(BF16)
        h_ref[u] = h
        b_ref[u] = scaled(h.astype(F32), gain_m_ref[...])

    def mlp(b):
        gate, up = dot(b, wg_ref[...]), dot(b, wu_ref[...])
        return dot((jax.nn.silu(gate) * up).astype(BF16), wd_ref[...])

    def finish(u):
        y_ref[u] = (h_ref[u].astype(F32) + summed(1, u)).astype(BF16)

    def mlp_of_two(u):
        term = mlp(b_ref[pl.ds(u, 2)].astype(F32).reshape(2 * UNIT, d).astype(BF16))
        send_terms(1, u, term[:UNIT])
        send_terms(1, u + 1, term[UNIT:])

    def step(u, carry):
        for c in (0, 1):
            chunk(u, c).wait()
        for i, block in enumerate(score(u, (0, 1))):
            s_ref[:, i * BLOCK:(i + 1) * BLOCK] = block
        for c in (0, 1):
            refill(u, c)
        weigh()

        @pl.when(u == 0)
        def _():
            copies[len(early) - 1].wait()

        @pl.when(u == 2)
        def _():
            for copy in copies[len(early):]:
                copy.wait()

        @pl.when(u == 5)
        def _():
            send_sums(1, u - 5)
            send_sums(1, u - 4)

        for c in (2, 3):
            chunk(u, c).wait()
        project(u, mixed(u, (2, 3)))
        for c in (2, 3):
            refill(u, c)

        @pl.when(u > 0)
        def _():
            send_sums(0, u - 1)

        @pl.when(u == 6)
        def _():
            send_sums(1, u - 4)
            send_sums(1, u - 3)

        @pl.when(u > 1)
        def _():
            middle(u - 2)

        @pl.when((u == 3) | (u == 5))
        def _():
            mlp_of_two(u - 3)

        return carry

    lax.fori_loop(0, units - 1, step, 0)

    e, f = units - 2, units - 1
    for c in (0, 1):
        chunk(f, c).wait()
        for i, block in enumerate(score(f, (c,))):
            at = slice(i * BLOCK, (i + 1) * BLOCK)
            s_ref[:, at] = block + s_ref[:, at] if c else block
    weigh()
    chunk(f, 2).wait()
    part_o[...] = mixed(f, (2,))
    chunk(f, 3).wait()
    project(f, part_o[...] + mixed(f, (3,)))

    def sent(n, u):
        landed(first, n, u, 0, send_sem)
        landed(second, n, u, 1, send_sem)

    def drain(u, carry):
        sent(0, u)
        sent(1, u)
        return carry

    send_sums(0, e)
    middle(e - 1)
    mlp_of_two(e - 2)
    for u in range(e - 4):
        finish(u)
    send_sums(0, f)
    middle(e)
    send_terms(1, e, mlp(b_ref[e]))
    send_sums(1, e - 2)
    send_sums(1, e - 1)
    middle(f)
    send_terms(1, f, mlp(b_ref[f]))
    for u in range(e - 4, e - 2):
        finish(u)
    send_sums(1, e)
    lax.fori_loop(0, e - 2, drain, 0)
    finish(e - 2)
    finish(e - 1)
    send_sums(1, f)
    lax.fori_loop(e - 2, e, drain, 0)
    sent(0, e)
    sent(0, f)
    finish(e)
    sent(1, e)
    finish(f)
    sent(1, f)


def turn_table(cache):
    half = HEAD // 2
    angle = (cache - 1) * float(THETA) ** (-np.arange(half) / half)
    cos, sin = np.cos(angle), np.sin(angle)
    table = np.zeros((8, HEAD), np.float32)
    table[0] = np.concatenate([cos, cos])
    table[1] = np.concatenate([-sin, sin])
    return table


def solution(mesh):
    devices = mesh.shape["tp"]
    side = int(devices**0.5)

    def step(x, k_cache, v_cache, gain_a, wq, wo, gain_m, w_gate, w_up, w_down):
        batch, cache = k_cache.shape[:2]
        d = x.shape[1]
        units = batch // UNIT
        hbm = pl.BlockSpec(memory_space=pltpu.HBM)
        operands = (
            x.reshape(units, UNIT, d), gain_a, gain_m, turn_table(cache),
            wq, wo, w_gate, w_up, w_down, k_cache.reshape(batch * cache, HEAD), v_cache.reshape(batch * cache, HEAD),
        )
        buffers = pltpu.VMEM((2, units, 2 * side, UNIT, d // 2), BF16)
        y = pl.pallas_call(
            functools.partial(layer, side, cache),
            name="layer",
            out_shape=jax.ShapeDtypeStruct((units, UNIT, d), BF16),
            in_specs=[hbm] * len(operands),
            out_specs=pl.BlockSpec(memory_space=pltpu.VMEM),
            scratch_shapes=[pltpu.VMEM(t.shape, t.dtype) for t in operands[:-2]] + [
                pltpu.VMEM((AHEAD * CHUNKS, PART * cache, HEAD), BF16),
                pltpu.VMEM((units, UNIT, UNIT * HEAD), BF16),
                pltpu.VMEM((UNIT, cache), F32),
                pltpu.VMEM((UNIT, cache), BF16),
                pltpu.VMEM((UNIT, HEAD), F32),
                pltpu.VMEM((units, UNIT, d), BF16),
                pltpu.VMEM((units, UNIT, d), BF16),
                buffers,
                buffers,
                pltpu.SemaphoreType.DMA((len(operands) - 2,)),
                pltpu.SemaphoreType.DMA((AHEAD * CHUNKS,)),
                pltpu.SemaphoreType.DMA((2, units, 2)),
                pltpu.SemaphoreType.DMA((2, units, 2)),
            ],
            compiler_params=pltpu.CompilerParams(collective_id=0, has_side_effects=True, vmem_limit_bytes=58 * 2**20),
        )(*operands)
        return y.reshape(batch, d)

    states, cache, columns, rows_of = P("dp", None), P("dp", None, "tp", None), P(None, "tp"), P("tp", None)
    return jax.shard_map(
        step,
        mesh=mesh,
        in_specs=(states, cache, cache, P(None), columns, rows_of, P(None), columns, columns, rows_of),
        out_specs=states,
        check_vma=False,
    )
```

time: 77.2 us -> 66.9 us (0.87)
  Pallas kernels: 72.8 us -> 65.1 us
  local copies, waits for them, and re-layouts: 4.24 us -> 1.67 us
    pallas_call x1, Pallas kernels: 72.8 us -> 65.1 us  [step(): pl.pallas_call(functools.partial(layer, side, cache), name='layer', out_s...]
    reshape x2 -> x0, local copies, waits for them, and re-layouts: 2.57 us -> none  [the longest x1 1.29 us: step(): gain_a.reshape(1, d)]
where the time goes in v2:
time: 66.9 us; the launch traced here: 66.8 us
  Pallas kernels  65.1 us (97%)
  local copies, waits for them, and re-layouts  1.67 us (2%)
    pallas_call x1, Pallas kernels, step(): pl.pallas_call(functools.partial(layer, side, cache), name='layer', out_s...  65.1 us
    unnamed x1, local copies, waits for them, and re-layouts  1.67 us

profile of v2, /device:TPU:96, one launch (start us, length us, event | category | flops | bytes accessed | tf_op | source)
XLA Modules:
  0.0 66.8 jit_solution(13717031446203844454)
XLA Ops:
  0.0 65.1 %layer.1 = bf16[8,8,2048]{2,1,0:T(8,128)(2,1)} custom-call(bf16[8,8,2048]{2,1,0:T(8,128)(2,1)} %bitcast.5, bf16[2048]{0:T(1024)(128)(2,1)} %gain_a_hbm.1, bf16[2048]{0:T(1024)(128)(2,1)} %gain_m_hbm.1, f32[8,128]{1,0:T(8,128)} %constant.2.clone.turn_hbm, bf16[2048,128]{1,0:T(8,128)(2,1)} %wq_hbm.1, bf16[128,2048]{1,0:T(8,128)(2,1)} %wo_hbm.1, ...), custom_call_target="tpu_custom_call" | custom-call | tf_op jit(solution)/shard_map/layer/pallas_call | solution.py:288
  65.1 1.7 %copy.13 = bf16[64,2048]{1,0:T(8,128)(2,1)} copy(bf16[64,2048]{1,0:T(8,128)(2,1)} %bitcast.4) | data formatting | bytes 524288

commit v3 on v2

v3 whole, which is shorter than its diff:
```python
import functools

import jax
import jax.numpy as jnp
import numpy as np
from jax import lax
from jax.experimental import pallas as pl
from jax.experimental.pallas import tpu as pltpu
from jax.sharding import PartitionSpec as P

HEAD = 128
THETA = 10000
PART = 4
CHUNKS = 4
AHEAD = 2
BLOCK = 256
UNIT = 8


F32, BF16 = jnp.float32, jnp.bfloat16


def scaled(wide, gain):
    scale = lax.rsqrt(jnp.mean(wide * wide, -1, keepdims=True) + 1e-6)
    return (wide * scale * gain.astype(F32).reshape(1, -1)).astype(BF16)


def dot(a, b):
    return jnp.dot(a, b, preferred_element_type=F32)


def layer(
    side, cache,
    x_hbm, gain_a_hbm, gain_m_hbm, turn_hbm, wq_hbm, wo_hbm, wg_hbm, wu_hbm, wd_hbm, k_hbm, v_hbm,
    y_ref,
    x_ref, gain_a_ref, gain_m_ref, turn_ref, wq_ref, wo_ref, wg_ref, wu_ref, wd_ref,
    ring, qd, s_ref, p_ref, part_o, h_ref, b_ref, first, second, blocks,
    in_sem, ring_sem, send_sem, recv_sem, block_recv_sem,
):
    units, _, d = x_ref.shape
    batch = units * UNIT
    half = d // 2
    rows = PART * cache
    me = lax.axis_index("tp")
    mx, my = me // side, me % side
    hops = sorted(range(1, side), key=lambda i: -min(i, side - i))
    line_x = [(p, p * side + my) for p in (lax.rem(mx + i, side) for i in hops)]
    line_y = [(p, mx * side + p) for p in (lax.rem(my + i, side) for i in hops)]

    barrier = pltpu.get_barrier_semaphore()
    for _, peer in line_x + line_y:
        pl.semaphore_signal(barrier, inc=1, device_id={"tp": peer}, device_id_type=pl.DeviceIdType.MESH)

    def chunk(u, c):
        turn = lax.rem(u, AHEAD)
        slot = turn * CHUNKS + c
        src = (k_hbm, v_hbm)[c // 2].at[pl.ds((2 * u + c % 2) * rows, rows)]
        return src, ring.at[slot], ring_sem.at[slot], ring_sem.at[AHEAD * CHUNKS + turn]

    def started(u, c):
        src, dst, *sems = chunk(u, c)
        if c < CHUNKS - 1:
            pltpu.make_async_copy(src, dst, sems[0]).start()
            return
        for part in range(2):
            for i in range(PART):
                piece = pl.ds(i * cache + part * cache // 2, cache // 2)
                pltpu.make_async_copy(src.at[piece], dst.at[piece], sems[part]).start()

    def arrived(u, c, parts=(0, 1)):
        src, dst, *sems = chunk(u, c)
        if c < CHUNKS - 1:
            pltpu.make_async_copy(src, dst, sems[0]).wait()
            return
        for part in parts:
            size = pl.ds(0, rows // 2)
            pltpu.make_async_copy(src.at[size], dst.at[size], sems[part]).wait()

    def refill(u, c):
        @pl.when(u + AHEAD < units)
        def _():
            started(u + AHEAD, c)

    early = [(x_hbm, x_ref), (gain_a_hbm, gain_a_ref), (gain_m_hbm, gain_m_ref), (turn_hbm, turn_ref), (wq_hbm, wq_ref), (wo_hbm, wo_ref)]
    late = [(wg_hbm, wg_ref), (wu_hbm, wu_ref), (wd_hbm, wd_ref)]
    copies = [pltpu.make_async_copy(a, b, in_sem.at[i]) for i, (a, b) in enumerate(early + late)]
    for copy in copies[:len(early)]:
        copy.start()
    for c in range(2):
        started(0, c)
    for copy in copies[:len(early) - 1]:
        copy.wait()
    for t in range(2, AHEAD * CHUNKS):
        started(t // CHUNKS, t % CHUNKS)
    for copy in copies[len(early):]:
        copy.start()

    a = scaled(x_ref[...].astype(F32).reshape(batch, d), gain_a_ref[...])
    q = dot(a, wq_ref[...]).astype(BF16).astype(F32)
    q = q * turn_ref[0:1, :] + pltpu.roll(q, HEAD // 2, 1) * turn_ref[1:2, :]
    row = lax.broadcasted_iota(jnp.int32, (UNIT, HEAD), 0)
    for u in range(units):
        for i in range(UNIT):
            qd[u, :, i * HEAD:(i + 1) * HEAD] = jnp.where(row == i, q[u * UNIT:(u + 1) * UNIT], 0.0).astype(BF16)
    pl.semaphore_wait(barrier, 2 * (side - 1))

    def side_by_side(u, c, seqs, at):
        slot = lax.rem(u, AHEAD) * CHUNKS + c
        return jnp.concatenate([ring[slot + i // PART, pl.ds(i % PART * cache + at, BLOCK), :] for i in seqs], axis=1)

    def score(u, seqs):
        lhs = qd[u, :, seqs[0] * HEAD:(seqs[-1] + 1) * HEAD]
        return [
            lax.dot_general(lhs, side_by_side(u, 0, seqs, at), (((1,), (1,)), ((), ())), preferred_element_type=F32)
            for at in range(0, cache, BLOCK)
        ]

    def score_half(u, c):
        arrived(u, c)
        for i, block in enumerate(score(u, range(c * PART, (c + 1) * PART))):
            at = slice(i * BLOCK, (i + 1) * BLOCK)
            s_ref[:, at] = block + s_ref[:, at] if c else block

    def weigh():
        scores = s_ref[...] * HEAD**-0.5
        e = jnp.exp(scores - jnp.max(scores, -1, keepdims=True))
        p_ref[...] = (e * (1 / jnp.sum(e, -1, keepdims=True))).astype(BF16)

    def mixed(u, seqs, start=0, end=cache):
        acc = jnp.zeros((UNIT, len(seqs) * HEAD), F32)
        for at in range(start, end, BLOCK):
            acc += dot(p_ref[:, at:at + BLOCK], side_by_side(u, CHUNKS // 2, seqs, at))
        o = jnp.zeros((UNIT, HEAD), F32)
        for n, i in enumerate(seqs):
            o = jnp.where(row == i, acc[:, n * HEAD:(n + 1) * HEAD], o)
        return o

    def send(src, dst, send_sem, recv_sem, peer):
        pltpu.make_async_remote_copy(
            src_ref=src, dst_ref=dst, send_sem=send_sem, recv_sem=recv_sem,
            device_id={"tp": peer}, device_id_type=pl.DeviceIdType.MESH,
        ).start()

    def landed(slots, sem):
        all_of_it = slots.at[pl.ds(0, 2 * (side - 1))]
        pltpu.make_async_copy(all_of_it, all_of_it, sem).wait()

    def total(slots, start):
        t = slots[start].astype(F32)
        for i in range(1, side):
            t = t + slots[start + i].astype(F32)
        return t

    def spread(slots, sems, along_x, along_y, term):
        for slot, value in ((along_x, term[0]), (along_y, term[1])):
            slots[slot] = value.astype(BF16)
        for slot, line in ((along_x, line_x), (along_y, line_y)):
            for _, peer in line:
                send(slots.at[slot], slots.at[slot], *sems, peer)

    def sems(u, hop):
        return send_sem.at[hop], recv_sem.at[u, hop]

    def send_terms(u, term):
        spread(first.at[u], sems(u, 0), mx, side + my, (term[:, :half], term[:, half:]))

    def send_sums(u):
        landed(first.at[u], recv_sem.at[u, 0])
        spread(second.at[u], sems(u, 1), side + mx, my, (total(first.at[u], side), total(first.at[u], 0)))

    def summed(u):
        landed(second.at[u], recv_sem.at[u, 1])
        return jnp.concatenate([total(second.at[u], 0), total(second.at[u], side)], axis=1)

    def block_sems(u, hop):
        return send_sem.at[2], block_recv_sem.at[u, hop]

    def scatter(u, term):
        width = half // side
        out, slots = blocks.at[0, u], blocks.at[1, u]
        for i in range(2 * side):
            out[i] = term[:, i * width:(i + 1) * width].astype(BF16)
        for start, mine, line in ((0, mx, line_x), (side, my, line_y)):
            slots[start + mine] = out[start + mine]
            for p, peer in line:
                send(out.at[start + p], slots.at[start + mine], *block_sems(u, 0), peer)

    def across(u):
        slots = blocks.at[1, u]
        landed(slots, block_recv_sem.at[u, 0])
        spread(blocks.at[2, u], block_sems(u, 1), side + mx, my, (total(slots, side), total(slots, 0)))

    def gather(u):
        slots = blocks.at[2, u]
        landed(slots, block_recv_sem.at[u, 1])
        spread(blocks.at[3, u], block_sems(u, 2), mx, side + my, (total(slots, 0), total(slots, side)))

    def gathered(u):
        slots = blocks.at[3, u]
        landed(slots, block_recv_sem.at[u, 2])
        return jnp.concatenate([slots[i].astype(F32) for i in range(2 * side)], axis=1)

    def project(u, o):
        send_terms(u, dot(o.astype(BF16), wo_ref[...]))

    def middle(u):
        h = (x_ref[u].astype(F32) + summed(u)).astype(BF16)
        h_ref[u] = h
        b_ref[u] = scaled(h.astype(F32), gain_m_ref[...])

    def mlp(b):
        gate, up = dot(b, wg_ref[...]), dot(b, wu_ref[...])
        return dot((jax.nn.silu(gate) * up).astype(BF16), wd_ref[...])

    def finish(u, total):
        y_ref[u] = (h_ref[u].astype(F32) + total).astype(BF16)

    def mlp_of(u, n):
        term = mlp(b_ref[pl.ds(u, n)].astype(F32).reshape(n * UNIT, d).astype(BF16))
        for i in range(n):
            scatter(u + i, term[i * UNIT:(i + 1) * UNIT])

    def step(u, carry):
        for c in (0, 1):
            score_half(u, c)
            refill(u, c)
        weigh()

        @pl.when(u == 0)
        def _():
            copies[len(early) - 1].wait()

        @pl.when(u == 2)
        def _():
            for copy in copies[len(early):]:
                copy.wait()

        arrived(u, 2)
        part_o[...] = mixed(u, range(PART))
        refill(u, 2)
        arrived(u, 3)
        project(u, part_o[...] + mixed(u, range(PART, UNIT)))
        refill(u, 3)

        @pl.when(u > 0)
        def _():
            send_sums(u - 1)

        @pl.when((u > 1) & (u < units - 2))
        def _():
            middle(u - 2)

        @pl.when(u == 3)
        def _():
            mlp_of(u - 3, 2)

        return carry

    lax.fori_loop(0, units - 1, step, 0)

    e, f = units - 2, units - 1
    for c in (0, 1):
        score_half(f, c)
    weigh()
    arrived(f, 2)
    part_o[...] = mixed(f, range(PART))
    arrived(f, 3, (0,))
    part_o[...] += mixed(f, range(PART, UNIT), 0, cache // 2)
    arrived(f, 3, (1,))
    project(f, part_o[...] + mixed(f, range(PART, UNIT), cache // 2, cache))

    send_sums(e)
    middle(e - 2)
    middle(e - 1)
    mlp_of(e - 4, 4)
    send_sums(f)
    middle(e)
    scatter(e, mlp(b_ref[e]))
    for u in range(e):
        across(u)
    middle(f)
    send_terms(units, mlp(b_ref[f]))
    across(e)
    for u in range(e):
        gather(u)
    send_sums(units)
    gather(e)
    for u in range(e):
        finish(u, gathered(u))
    finish(f, summed(units))
    finish(e, gathered(e))

    others = pl.ds(0, 2 * (side - 1))
    for sem, sent in enumerate((first.at[:, others], second.at[:, others], blocks.at[pl.ds(0, 3), :, others])):
        pltpu.make_async_copy(sent, sent, send_sem.at[sem]).wait()


def turn_table(cache):
    half = HEAD // 2
    angle = (cache - 1) * float(THETA) ** (-np.arange(half) / half)
    cos, sin = np.cos(angle), np.sin(angle)
    table = np.zeros((8, HEAD), np.float32)
    table[0] = np.concatenate([cos, cos])
    table[1] = np.concatenate([-sin, sin])
    return table


def solution(mesh):
    devices = mesh.shape["tp"]
    side = int(devices**0.5)

    def step(x, k_cache, v_cache, gain_a, wq, wo, gain_m, w_gate, w_up, w_down):
        batch, cache = k_cache.shape[:2]
        d = x.shape[1]
        units = batch // UNIT
        hbm = pl.BlockSpec(memory_space=pltpu.HBM)
        operands = (
            x.reshape(units, UNIT, d), gain_a, gain_m, jnp.asarray(turn_table(cache)),
            wq, wo, w_gate, w_up, w_down, k_cache.reshape(batch * cache, HEAD), v_cache.reshape(batch * cache, HEAD),
        )
        operands = tuple(pltpu.with_memory_space_constraint(t, pltpu.HBM) for t in operands)
        buffers = pltpu.VMEM((units + 1, 2 * side, UNIT, d // 2), BF16)
        y = pl.pallas_call(
            functools.partial(layer, side, cache),
            name="layer",
            out_shape=jax.ShapeDtypeStruct((units, UNIT, d), BF16),
            in_specs=[hbm] * len(operands),
            out_specs=pl.BlockSpec(memory_space=pltpu.VMEM),
            scratch_shapes=[pltpu.VMEM(t.shape, t.dtype) for t in operands[:-2]] + [
                pltpu.VMEM((AHEAD * CHUNKS, PART * cache, HEAD), BF16),
                pltpu.VMEM((units, UNIT, UNIT * HEAD), BF16),
                pltpu.VMEM((UNIT, cache), F32),
                pltpu.VMEM((UNIT, cache), BF16),
                pltpu.VMEM((UNIT, HEAD), F32),
                pltpu.VMEM((units, UNIT, d), BF16),
                pltpu.VMEM((units, UNIT, d), BF16),
                buffers,
                buffers,
                pltpu.VMEM((4, units - 1, 2 * side, UNIT, d // 2 // side), BF16),
                pltpu.SemaphoreType.DMA((len(operands) - 2,)),
                pltpu.SemaphoreType.DMA((AHEAD * (CHUNKS + 1),)),
                pltpu.SemaphoreType.DMA((3,)),
                pltpu.SemaphoreType.DMA((units + 1, 2)),
                pltpu.SemaphoreType.DMA((units - 1, 3)),
            ],
            compiler_params=pltpu.CompilerParams(collective_id=0, has_side_effects=True, vmem_limit_bytes=52 * 2**20),
        )(*operands)
        return y.reshape(batch, d)

    states, cache, columns, rows_of = P("dp", None), P("dp", None, "tp", None), P(None, "tp"), P("tp", None)
    return jax.shard_map(
        step,
        mesh=mesh,
        in_specs=(states, cache, cache, P(None), columns, rows_of, P(None), columns, columns, rows_of),
        out_specs=states,
        check_vma=False,
    )
```

time: 66.9 us -> 63.9 us (0.955)
  Pallas kernels: 65.1 us -> 63.1 us
  local copies, waits for them, and re-layouts: 1.67 us -> 0.71 us
    pallas_call x1, Pallas kernels: 65.1 us -> 63.1 us  [step(): pl.pallas_call(functools.partial(layer, side, cache), name='layer', out_s...]
    unnamed x1, local copies, waits for them, and re-layouts: 1.67 us -> 0.71 us
where the time goes in v3:
time: 63.9 us; the launch traced here: 63.8 us
  Pallas kernels  63.1 us (99%)
  local copies, waits for them, and re-layouts  0.71 us (1%)
    pallas_call x1, Pallas kernels, step(): pl.pallas_call(functools.partial(layer, side, cache), name='layer', out_s...  63.1 us

profile of v3, /device:TPU:96, one launch (start us, length us, event | category | flops | bytes accessed | tf_op | source)
XLA Modules:
  0.0 63.8 jit_solution(5225996923498381840)
XLA Ops:
  0.0 63.1 %layer.1 = bf16[8,8,2048]{2,1,0:T(8,128)(2,1)S(1)} custom-call(bf16[8,8,2048]{2,1,0:T(8,128)(2,1)} %bitcast.5, bf16[2048]{0:T(1024)(128)(2,1)} %gain_a_hbm.1, bf16[2048]{0:T(1024)(128)(2,1)} %gain_m_hbm.1, f32[8,128]{1,0:T(8,128)} %constant.2.clone.turn_hbm, bf16[2048,128]{1,0:T(8,128)(2,1)} %wq_hbm.1, bf16[128,2048]{1,0:T(8,128)(2,1)} %wo_hbm.1, ...), custom_call_target="tpu_custom_call" | custom-call | tf_op jit(solution)/shard_map/layer/pallas_call | solution.py:323
  63.1 0.7 %copy.13 = bf16[64,2048]{1,0:T(8,128)(2,1)} copy(bf16[64,2048]{1,0:T(8,128)(2,1)S(1)} %bitcast.4) | data formatting | bytes 524288

commit v4 on v3

--- a/solution.py
+++ b/solution.py
@@ -34,8 +34,8 @@
     x_hbm, gain_a_hbm, gain_m_hbm, turn_hbm, wq_hbm, wo_hbm, wg_hbm, wu_hbm, wd_hbm, k_hbm, v_hbm,
     y_ref,
     x_ref, gain_a_ref, gain_m_ref, turn_ref, wq_ref, wo_ref, wg_ref, wu_ref, wd_ref,
-    ring, qd, s_ref, p_ref, part_o, h_ref, b_ref, first, second, blocks,
-    in_sem, ring_sem, send_sem, recv_sem, block_recv_sem,
+    ring, qd, s_ref, p_ref, part_o, h_ref, b_ref, first, second, dealt,
+    in_sem, ring_sem, send_sem, recv_sem, deal_recv_sem,
 ):
     units, _, d = x_ref.shape
     batch = units * UNIT
@@ -44,11 +44,13 @@
     me = lax.axis_index("tp")
     mx, my = me // side, me % side
     hops = sorted(range(1, side), key=lambda i: -min(i, side - i))
-    line_x = [(p, p * side + my) for p in (lax.rem(mx + i, side) for i in hops)]
-    line_y = [(p, mx * side + p) for p in (lax.rem(my + i, side) for i in hops)]
+    line_x = [lax.rem(mx + i, side) * side + my for i in hops]
+    line_y = [mx * side + lax.rem(my + i, side) for i in hops]
 
     barrier = pltpu.get_barrier_semaphore()
-    for _, peer in line_x + line_y:
+    everyone = sorted(((i, j) for i in range(side) for j in range(side)), key=lambda t: -sum(min(i, side - i) for i in t))[:-1]
+    everyone = [lax.rem(mx + i, side) * side + lax.rem(my + j, side) for i, j in everyone]
+    for peer in everyone:
         pl.semaphore_signal(barrier, inc=1, device_id={"tp": peer}, device_id_type=pl.DeviceIdType.MESH)
 
     def chunk(u, c):
@@ -92,8 +94,6 @@
         copy.wait()
     for t in range(2, AHEAD * CHUNKS):
         started(t // CHUNKS, t % CHUNKS)
-    for copy in copies[len(early):]:
-        copy.start()
 
     a = scaled(x_ref[...].astype(F32).reshape(batch, d), gain_a_ref[...])
     q = dot(a, wq_ref[...]).astype(BF16).astype(F32)
@@ -102,7 +102,7 @@
     for u in range(units):
         for i in range(UNIT):
             qd[u, :, i * HEAD:(i + 1) * HEAD] = jnp.where(row == i, q[u * UNIT:(u + 1) * UNIT], 0.0).astype(BF16)
-    pl.semaphore_wait(barrier, 2 * (side - 1))
+    pl.semaphore_wait(barrier, len(everyone))
 
     def side_by_side(u, c, seqs, at):
         slot = lax.rem(u, AHEAD) * CHUNKS + c
@@ -155,7 +155,7 @@
         for slot, value in ((along_x, term[0]), (along_y, term[1])):
             slots[slot] = value.astype(BF16)
         for slot, line in ((along_x, line_x), (along_y, line_y)):
-            for _, peer in line:
+            for peer in line:
                 send(slots.at[slot], slots.at[slot], *sems, peer)
 
     def sems(u, hop):
@@ -172,33 +172,30 @@
         landed(second.at[u], recv_sem.at[u, 1])
         return jnp.concatenate([total(second.at[u], 0), total(second.at[u], side)], axis=1)
 
-    def block_sems(u, hop):
-        return send_sem.at[2], block_recv_sem.at[u, hop]
-
-    def scatter(u, term):
-        width = half // side
-        out, slots = blocks.at[0, u], blocks.at[1, u]
-        for i in range(2 * side):
-            out[i] = term[:, i * width:(i + 1) * width].astype(BF16)
-        for start, mine, line in ((0, mx, line_x), (side, my, line_y)):
-            slots[start + mine] = out[start + mine]
-            for p, peer in line:
-                send(out.at[start + p], slots.at[start + mine], *block_sems(u, 0), peer)
-
-    def across(u):
-        slots = blocks.at[1, u]
-        landed(slots, block_recv_sem.at[u, 0])
-        spread(blocks.at[2, u], block_sems(u, 1), side + mx, my, (total(slots, side), total(slots, 0)))
-
-    def gather(u):
-        slots = blocks.at[2, u]
-        landed(slots, block_recv_sem.at[u, 1])
-        spread(blocks.at[3, u], block_sems(u, 2), mx, side + my, (total(slots, 0), total(slots, side)))
-
-    def gathered(u):
-        slots = blocks.at[3, u]
-        landed(slots, block_recv_sem.at[u, 2])
-        return jnp.concatenate([slots[i].astype(F32) for i in range(2 * side)], axis=1)
+    def deal():
+        slots = dealt.at[1]
+        slots[me] = dealt[0, me]
+        for peer in everyone:
+            send(dealt.at[0, peer], slots.at[me], send_sem.at[2], deal_recv_sem.at[0], peer)
+
+    def waited(slots, sem):
+        rest = slots.at[pl.ds(0, side * side - 1)]
+        pltpu.make_async_copy(rest, rest, sem).wait()
+
+    def settle():
+        slots, sums = dealt.at[1], dealt.at[2]
+        waited(slots, deal_recv_sem.at[0])
+        t = slots[0].astype(F32)
+        for i in range(1, side * side):
+            t = t + slots[i].astype(F32)
+        sums[me] = t.astype(BF16)
+        for peer in everyone:
+            send(sums.at[me], sums.at[me], send_sem.at[3], deal_recv_sem.at[1], peer)
+
+    def settled():
+        sums = dealt.at[2]
+        waited(sums, deal_recv_sem.at[1])
+        return jnp.concatenate([sums[i].astype(F32) for i in range(side * side)], axis=1)
 
     def project(u, o):
         send_terms(u, dot(o.astype(BF16), wo_ref[...]))
@@ -214,11 +211,6 @@
 
     def finish(u, total):
         y_ref[u] = (h_ref[u].astype(F32) + total).astype(BF16)
-
-    def mlp_of(u, n):
-        term = mlp(b_ref[pl.ds(u, n)].astype(F32).reshape(n * UNIT, d).astype(BF16))
-        for i in range(n):
-            scatter(u + i, term[i * UNIT:(i + 1) * UNIT])
 
     def step(u, carry):
         for c in (0, 1):
@@ -229,11 +221,6 @@
         @pl.when(u == 0)
         def _():
             copies[len(early) - 1].wait()
-
-        @pl.when(u == 2)
-        def _():
-            for copy in copies[len(early):]:
-                copy.wait()
 
         arrived(u, 2)
         part_o[...] = mixed(u, range(PART))
@@ -249,10 +236,6 @@
         @pl.when((u > 1) & (u < units - 2))
         def _():
             middle(u - 2)
-
-        @pl.when(u == 3)
-        def _():
-            mlp_of(u - 3, 2)
 
         return carry
 
@@ -267,31 +250,36 @@
     arrived(f, 3, (0,))
     part_o[...] += mixed(f, range(PART, UNIT), 0, cache // 2)
     arrived(f, 3, (1,))
+    for copy in copies[len(early):]:
+        copy.start()
     project(f, part_o[...] + mixed(f, range(PART, UNIT), cache // 2, cache))
 
     send_sums(e)
     middle(e - 2)
     middle(e - 1)
-    mlp_of(e - 4, 4)
+    for copy in copies[len(early):]:
+        copy.wait()
+    term = mlp(b_ref[pl.ds(0, e)].astype(F32).reshape(e * UNIT, d).astype(BF16))
+    width = d // (side * side)
+    for i in range(side * side):
+        dealt[0, i] = term[:, i * width:(i + 1) * width].astype(BF16)
     send_sums(f)
+    deal()
     middle(e)
-    scatter(e, mlp(b_ref[e]))
+    send_terms(units, mlp(b_ref[e]))
+    middle(f)
+    send_terms(units + 1, mlp(b_ref[f]))
+    settle()
+    send_sums(units)
+    send_sums(units + 1)
+    finish(e, summed(units))
+    t = settled()
     for u in range(e):
-        across(u)
-    middle(f)
-    send_terms(units, mlp(b_ref[f]))
-    across(e)
-    for u in range(e):
-        gather(u)
-    send_sums(units)
-    gather(e)
-    for u in range(e):
-        finish(u, gathered(u))
-    finish(f, summed(units))
-    finish(e, gathered(e))
-
-    others = pl.ds(0, 2 * (side - 1))
-    for sem, sent in enumerate((first.at[:, others], second.at[:, others], blocks.at[pl.ds(0, 3), :, others])):
+        finish(u, t[u * UNIT:(u + 1) * UNIT])
+    finish(f, summed(units + 1))
+
+    others, rest = pl.ds(0, 2 * (side - 1)), pl.ds(0, side * side - 1)
+    for sem, sent in enumerate((first.at[:, others], second.at[:, others], dealt.at[0, rest], dealt.at[2, rest])):
         pltpu.make_async_copy(sent, sent, send_sem.at[sem]).wait()
 
 
@@ -319,7 +307,7 @@
             wq, wo, w_gate, w_up, w_down, k_cache.reshape(batch * cache, HEAD), v_cache.reshape(batch * cache, HEAD),
         )
         operands = tuple(pltpu.with_memory_space_constraint(t, pltpu.HBM) for t in operands)
-        buffers = pltpu.VMEM((units + 1, 2 * side, UNIT, d // 2), BF16)
+        buffers = pltpu.VMEM((units + 2, 2 * side, UNIT, d // 2), BF16)
         y = pl.pallas_call(
             functools.partial(layer, side, cache),
             name="layer",
@@ -336,12 +324,12 @@
                 pltpu.VMEM((units, UNIT, d), BF16),
                 buffers,
                 buffers,
-                pltpu.VMEM((4, units - 1, 2 * side, UNIT, d // 2 // side), BF16),
+                pltpu.VMEM((3, devices, (units - 2) * UNIT, d // devices), BF16),
                 pltpu.SemaphoreType.DMA((len(operands) - 2,)),
                 pltpu.SemaphoreType.DMA((AHEAD * (CHUNKS + 1),)),
-                pltpu.SemaphoreType.DMA((3,)),
-                pltpu.SemaphoreType.DMA((units + 1, 2)),
-                pltpu.SemaphoreType.DMA((units - 1, 3)),
+                pltpu.SemaphoreType.DMA((4,)),
+                pltpu.SemaphoreType.DMA((units + 2, 2)),
+                pltpu.SemaphoreType.DMA((2,)),
             ],
             compiler_params=pltpu.CompilerParams(collective_id=0, has_side_effects=True, vmem_limit_bytes=52 * 2**20),
         )(*operands)

time: 63.9 us -> 62.2 us (0.973)
  Pallas kernels: 63.1 us -> 61.4 us
    pallas_call x1, Pallas kernels: 63.1 us -> 61.4 us  [step(): pl.pallas_call(functools.partial(layer, side, cache), name='layer', out_s...]
where the time goes in v4:
time: 62.2 us; the launch traced here: 62.1 us
  Pallas kernels  61.4 us (99%)
  local copies, waits for them, and re-layouts  0.71 us (1%)
    pallas_call x1, Pallas kernels, step(): pl.pallas_call(functools.partial(layer, side, cache), name='layer', out_s...  61.4 us

profile of v4, /device:TPU:96, one launch (start us, length us, event | category | flops | bytes accessed | tf_op | source)
XLA Modules:
  0.0 62.1 jit_solution(14952072315272040956)
XLA Ops:
  0.0 61.4 %layer.1 = bf16[8,8,2048]{2,1,0:T(8,128)(2,1)S(1)} custom-call(bf16[8,8,2048]{2,1,0:T(8,128)(2,1)} %bitcast.5, bf16[2048]{0:T(1024)(128)(2,1)} %gain_a_hbm.1, bf16[2048]{0:T(1024)(128)(2,1)} %gain_m_hbm.1, f32[8,128]{1,0:T(8,128)} %constant.2.clone.turn_hbm, bf16[2048,128]{1,0:T(8,128)(2,1)} %wq_hbm.1, bf16[128,2048]{1,0:T(8,128)(2,1)} %wo_hbm.1, ...), custom_call_target="tpu_custom_call" | custom-call | tf_op jit(solution)/shard_map/layer/pallas_call | solution.py:311
  61.4 0.7 %copy.13 = bf16[64,2048]{1,0:T(8,128)(2,1)} copy(bf16[64,2048]{1,0:T(8,128)(2,1)S(1)} %bitcast.4) | data formatting | bytes 524288

commit v5 on v4

--- a/solution.py
+++ b/solution.py
@@ -12,6 +12,7 @@
 THETA = 10000
 PART = 4
 CHUNKS = 4
+TURNS = 4
 AHEAD = 2
 BLOCK = 256
 UNIT = 8
@@ -85,7 +86,8 @@
 
     early = [(x_hbm, x_ref), (gain_a_hbm, gain_a_ref), (gain_m_hbm, gain_m_ref), (turn_hbm, turn_ref), (wq_hbm, wq_ref), (wo_hbm, wo_ref)]
     late = [(wg_hbm, wg_ref), (wu_hbm, wu_ref), (wd_hbm, wd_ref)]
-    copies = [pltpu.make_async_copy(a, b, in_sem.at[i]) for i, (a, b) in enumerate(early + late)]
+    in_sems = [ring_sem.at[2 + i] for i in range(len(early) - 1)] + [in_sem.at[i] for i in range(len(late) + 1)]
+    copies = [pltpu.make_async_copy(a, b, sem) for (a, b), sem in zip(early + late, in_sems)]
     for copy in copies[:len(early)]:
         copy.start()
     for c in range(2):
@@ -158,18 +160,21 @@
             for peer in line:
                 send(slots.at[slot], slots.at[slot], *sems, peer)
 
+    def turn(u):
+        return u - units + TURNS if isinstance(u, int) and u >= units else lax.rem(u, TURNS)
+
     def sems(u, hop):
-        return send_sem.at[hop], recv_sem.at[u, hop]
+        return send_sem.at[hop], recv_sem.at[turn(u), hop]
 
     def send_terms(u, term):
         spread(first.at[u], sems(u, 0), mx, side + my, (term[:, :half], term[:, half:]))
 
     def send_sums(u):
-        landed(first.at[u], recv_sem.at[u, 0])
+        landed(first.at[u], recv_sem.at[turn(u), 0])
         spread(second.at[u], sems(u, 1), side + mx, my, (total(first.at[u], side), total(first.at[u], 0)))
 
     def summed(u):
-        landed(second.at[u], recv_sem.at[u, 1])
+        landed(second.at[u], recv_sem.at[turn(u), 1])
         return jnp.concatenate([total(second.at[u], 0), total(second.at[u], side)], axis=1)
 
     def deal():
@@ -325,10 +330,10 @@
                 buffers,
                 buffers,
                 pltpu.VMEM((3, devices, (units - 2) * UNIT, d // devices), BF16),
-                pltpu.SemaphoreType.DMA((len(operands) - 2,)),
+                pltpu.SemaphoreType.DMA((4,)),
                 pltpu.SemaphoreType.DMA((AHEAD * (CHUNKS + 1),)),
                 pltpu.SemaphoreType.DMA((4,)),
-                pltpu.SemaphoreType.DMA((units + 2, 2)),
+                pltpu.SemaphoreType.DMA((TURNS + 2, 2)),
                 pltpu.SemaphoreType.DMA((2,)),
             ],
             compiler_params=pltpu.CompilerParams(collective_id=0, has_side_effects=True, vmem_limit_bytes=52 * 2**20),

time: 62.2 us -> 62 us (level)
  no operation moved by 1% of the time
where the time goes in v5:
time: 62 us
  Pallas kernels  61.3 us (99%)
  local copies, waits for them, and re-layouts  0.71 us (1%)
    pallas_call x1, Pallas kernels, step(): pl.pallas_call(functools.partial(layer, side, cache), name='layer', out_s...  61.3 us

profile of v5, /device:TPU:96, one launch (start us, length us, event | category | flops | bytes accessed | tf_op | source)
XLA Modules:
  0.0 62.0 jit_solution(2917728787469854766)
XLA Ops:
  0.0 61.3 %layer.1 = bf16[8,8,2048]{2,1,0:T(8,128)(2,1)S(1)} custom-call(bf16[8,8,2048]{2,1,0:T(8,128)(2,1)} %bitcast.5, bf16[2048]{0:T(1024)(128)(2,1)} %gain_a_hbm.1, bf16[2048]{0:T(1024)(128)(2,1)} %gain_m_hbm.1, f32[8,128]{1,0:T(8,128)} %constant.2.clone.turn_hbm, bf16[2048,128]{1,0:T(8,128)(2,1)} %wq_hbm.1, bf16[128,2048]{1,0:T(8,128)(2,1)} %wo_hbm.1, ...), custom_call_target="tpu_custom_call" | custom-call | tf_op jit(solution)/shard_map/layer/pallas_call | solution.py:316
  61.3 0.7 %copy.13 = bf16[64,2048]{1,0:T(8,128)(2,1)} copy(bf16[64,2048]{1,0:T(8,128)(2,1)S(1)} %bitcast.4) | data formatting | bytes 524288
